TPU v7x, 128 devices: a whole 4x4x4 slice. The times are simulated.
128 devices in a mesh: tm: 2 (over z_lo), grid: 64 (over z_hi, y, x, core).
Axes of the slice: x: 4, y: 4, z: 4 (z_hi: 2, z_lo: 2; z = z_hi * 2 + z_lo), core: 2. Of those that a mesh axis runs over, the one named last changes fastest.
Arguments:
- occupied_green: bfloat16 [2, 1024, 1024], P('tm', 'grid'), may hold values from -0.005859375 to 0.005859375
- empty_green: bfloat16 [2, 1024, 1024], P('tm', 'grid'), may hold values from -0.005859375 to 0.005859375
- basis: bfloat16 [12288, 1024], P('grid'), may hold values from -8 to 8
- time_weights: float32 [2, 2], replicated, may hold values from 0.25 to 1
Outputs:
- polarizability: float32 [2, 1024, 1024], P('tm', 'grid')
All inputs are finite; a program needn't handle non-finite values.
Results may differ from a plain program's by a relative error of at most 0.0012.
Values may be sent and summed in bfloat16 or wider, within the bound.
No kernel may reach another device: no remote copies, remote signals or barrier semaphores. Data moves between devices by JAX's collectives and lax.ppermute only.
A program may use at most 128 MiB of HBM per device.

v0:
```python
import jax
import jax.numpy as jnp
from jax import lax
from jax.sharding import Mesh
from jax.sharding import PartitionSpec as P

NR = 12288
NB = 1024
GRID = ("grid_0", "grid_1", "grid_2", "grid_3")


def cut_along(x, dim, devices):
    shape = x.shape
    tiles = x.reshape(*shape[:dim], devices, shape[dim] // devices, *shape[dim + 1 :])
    return jnp.moveaxis(tiles, dim, 0)


def laid_out(tiles, dim):
    shape = list(tiles.shape[1:])
    shape[dim] *= tiles.shape[0]
    return jnp.moveaxis(tiles, 0, dim).reshape(shape)


def moved_by_axis(tiles, axes, order):
    shape = [lax.axis_size(a) for a in axes]
    tiles = tiles.reshape(*shape, *tiles.shape[1:])
    for k in order:
        tiles = lax.all_to_all(tiles, axes[k], split_axis=k, concat_axis=k, tiled=True)
    return tiles.reshape(-1, *tiles.shape[len(axes) :])


def two_step_exchange(x, groups, order, split_dim, concat_dim):
    devices = lax.axis_size(groups[0]) * lax.axis_size(groups[1])
    tiles = cut_along(x, split_dim, devices)
    return laid_out(moved_by_axis(tiles, groups, order), concat_dim)


def sent_and_summed(x, axis, dim):
    tiles = cut_along(x, dim, lax.axis_size(axis))
    arrived = lax.all_to_all(tiles, axis, split_axis=0, concat_axis=0, tiled=True)
    return arrived.sum(axis=0)


def weigh_times(time_weights, block_list, scale_factor):
    time_count = len(block_list)
    group_index = lax.axis_index("tm")
    weights_local = lax.dynamic_slice_in_dim(time_weights, group_index * time_count, time_count, 1)
    accum = weights_local[:, 0, None, None] * block_list[0][None]
    return scale_factor * accum


def step_size(piece_rows):
    return max((divisor for divisor in range(1, 2049) if piece_rows % divisor == 0))


def shards(occupied_green, empty_green, basis, time_weights):
    stacked = jnp.stack([occupied_green, empty_green])
    time_count = occupied_green.shape[0]
    row_total = basis.shape[0]
    scale_factor = 1.0 / NR

    def make_accumulate(combined_rows):

        def accumulate(running, basis_piece, first_row):
            piece_rows = basis_piece.shape[0]
            step_rows = step_size(piece_rows)

            def one_step(step_index, inner):
                basis_subpart = lax.dynamic_slice_in_dim(
                    basis_piece, step_index * step_rows, step_rows, 0
                )
                real_pair = jnp.einsum(
                    "qoa,ba->qob", combined_rows, basis_subpart, preferred_element_type=jnp.float32
                )
                product = (real_pair[0] * real_pair[1]).astype(jnp.bfloat16)
                return inner + jnp.dot(product, basis_subpart, preferred_element_type=jnp.float32)

            return lax.fori_loop(0, piece_rows // step_rows, one_step, running)

        return accumulate

    initial = jnp.zeros((time_count * row_total, NB), jnp.float32)
    projected = jnp.einsum(
        "sl,ftkl->ftsk",
        basis,
        lax.all_gather(stacked, GRID, axis=2, tiled=True),
        preferred_element_type=jnp.float32,
    ).astype(jnp.bfloat16)
    combined_rows = projected.reshape(2, time_count * row_total, NB)
    accumulate = make_accumulate(combined_rows)
    summed = accumulate(initial, lax.all_gather(basis, GRID, axis=0, tiled=True), jnp.int32(0))
    back_half = summed.astype(jnp.bfloat16).reshape(time_count, row_total, NB)
    columns = two_step_exchange(back_half, (("grid_0", "grid_1", "grid_2"), "grid_3"), (1, 0), 2, 1)
    coef_cols = jnp.einsum(
        "tsk,sl->tkl",
        columns,
        lax.all_gather(basis, GRID, axis=0, tiled=True),
        preferred_element_type=jnp.float32,
    )
    block_list = [coef_cols[0]]
    result = sent_and_summed(weigh_times(time_weights, block_list, scale_factor), "tm", 0)
    return result


def solution(mesh):
    split = Mesh(
        mesh.devices.reshape(mesh.shape["tm"], 2, 4, 4, 2),
        ("tm", "grid_0", "grid_1", "grid_2", "grid_3"),
    )
    in_specs = (P("tm", GRID, None), P("tm", GRID, None), P(GRID, None), P())
    out_specs = P("tm", GRID, None)
    return jax.shard_map(
        shards, mesh=split, in_specs=in_specs, out_specs=out_specs, check_vma=False
    )
```

profile of v0, /device:TPU:0, one launch (start us, length us, event | category | flops | bytes accessed | tf_op | source)
XLA Modules:
  0.0 312.2 jit_solution(397094787537150573)
XLA Ops:
  6.5 0.0 copy-start
  6.5 0.0 all-gather.5.cloned.1.call-start
  6.5 1.4 pad_maximum_fusion
  8.0 0.0 all-gather.5.cloned.1.call-update
  8.0 0.0 all-gather.3.cloned.1.call-start
  8.0 0.7 all-gather.3.cloned.1.call-update
  8.7 77.5 %all-gather.5.cloned.1.call-done = bf16[2,1,1024,1024]{3,2,0,1:T(8,128)(2,1)} async-done(((bf16[2,1,16,1024]{3,2,0,1:T(8,128)(2,1)}), bf16[2,1,1024,1024]{3,2,0,1:T(8,128)(2,1)}) %all-gather.5.cloned.1.call-update) | async-done | bytes 4194320 | tf_op jit(solution)/shard_map/all_gather | solution.py:86
  86.2 3.8 %fusion.21 = bf16[2,192,1024]{2,1,0:T(8,128)(2,1)S(1)} fusion(bf16[2,1,1024,1024]{3,2,0,1:T(8,128)(2,1)} %all-gather.5.cloned.1.call-done, bf16[192,1024]{1,0:T(8,128)(2,1)} %param.8), kind=kOutput, calls=%fused_computation.15 | convolution fusion | flops 805699584 | bytes 5373952 | tf_op jit(solution)/shard_map/sl,ftkl->ftsk/dot_general | solution.py:83
  90.0 127.6 %all-gather.3.cloned.1.call-done = bf16[12288,1024]{1,0:T(8,128)(2,1)} async-done(((bf16[192,1024]{1,0:T(8,128)(2,1)}), bf16[12288,1024]{1,0:T(8,128)(2,1)}) %all-gather.3.cloned.1.call-update) | async-done | bytes 25165840 | tf_op jit(solution)/shard_map/all_gather | solution.py:91
  217.6 44.7 %while.14 = (s32[]{:T(128)}, f32[192,1024]{1,0:T(8,128)S(1)}, bf16[12288,1024]{1,0:T(8,128)(2,1)}, bf16[2,192,1024]{2,1,0:T(8,128)(2,1)S(1)}, s32[]{:T(128)}, /*index=5*/s32[]{:T(128)}, s32[]{:T(128)}, s32[]{:T(128)}) while((s32[]{:T(128)}, f32[192,1024]{1,0:T(8,128)S(1)}, bf16[12288,1024]{1,0:T(8,128)(2,1)}, ...), condition=%wide.region_1.0_spmd.clone, body=%wide.region_0.0_spmd.clone.sunk | while | flops 2417098752 | bytes 17039516 | solution.py:78
  217.6 4.0 %fusion.39 = f32[2,192,2048]{2,1,0:T(8,128)S(1)} fusion(bf16[2,192,1024]{2,1,0:T(8,128)(2,1)S(1)} %get-tuple-element.152, bf16[12288,1024]{1,0:T(8,128)(2,1)} %get-tuple-element.151, s32[]{:T(128)S(6)} %select_n.13), kind=kOutput, calls=%fused_computation.5.clone.1 | convolution fusion | flops 1610612736 | bytes 8126468 | tf_op jit(solution)/shard_map/while/body/eval_jaxpr/qoa,ba->qob/dot_general | solution.py:72
  221.6 3.4 %fusion.40 = f32[192,1024]{1,0:T(8,128)S(1)} fusion(bf16[12288,1024]{1,0:T(8,128)(2,1)} %get-tuple-element.151, s32[]{:T(128)S(6)} %select_n.13, f32[2,192,2048]{2,1,0:T(8,128)S(1)} %fusion.39, f32[192,1024]{1,0:T(8,128)S(1)} %get-tuple-element.142, pred[]{:T(512)S(6)} %compare.3), kind=kOutput, calls=%fused_computation.8.clone.1 | convolution fusion | flops 806486016 | bytes 8912901 | tf_op jit(solution)/shard_map/while/body/eval_jaxpr/dot_general | solution.py:76
  225.0 4.0 %fusion.39 = f32[2,192,2048]{2,1,0:T(8,128)S(1)} fusion(bf16[2,192,1024]{2,1,0:T(8,128)(2,1)S(1)} %get-tuple-element.152, bf16[12288,1024]{1,0:T(8,128)(2,1)} %get-tuple-element.151, s32[]{:T(128)S(6)} %select_n.13), kind=kOutput, calls=%fused_computation.5.clone.1 | convolution fusion | flops 1610612736 | bytes 8126468 | tf_op jit(solution)/shard_map/while/body/eval_jaxpr/qoa,ba->qob/dot_general | solution.py:72
  229.0 3.4 %fusion.40 = f32[192,1024]{1,0:T(8,128)S(1)} fusion(bf16[12288,1024]{1,0:T(8,128)(2,1)} %get-tuple-element.151, s32[]{:T(128)S(6)} %select_n.13, f32[2,192,2048]{2,1,0:T(8,128)S(1)} %fusion.39, f32[192,1024]{1,0:T(8,128)S(1)} %get-tuple-element.142, pred[]{:T(512)S(6)} %compare.3), kind=kOutput, calls=%fused_computation.8.clone.1 | convolution fusion | flops 806486016 | bytes 8912901 | tf_op jit(solution)/shard_map/while/body/eval_jaxpr/dot_general | solution.py:76
  232.5 4.0 %fusion.39 = f32[2,192,2048]{2,1,0:T(8,128)S(1)} fusion(bf16[2,192,1024]{2,1,0:T(8,128)(2,1)S(1)} %get-tuple-element.152, bf16[12288,1024]{1,0:T(8,128)(2,1)} %get-tuple-element.151, s32[]{:T(128)S(6)} %select_n.13), kind=kOutput, calls=%fused_computation.5.clone.1 | convolution fusion | flops 1610612736 | bytes 8126468 | tf_op jit(solution)/shard_map/while/body/eval_jaxpr/qoa,ba->qob/dot_general | solution.py:72
  236.5 3.4 %fusion.40 = f32[192,1024]{1,0:T(8,128)S(1)} fusion(bf16[12288,1024]{1,0:T(8,128)(2,1)} %get-tuple-element.151, s32[]{:T(128)S(6)} %select_n.13, f32[2,192,2048]{2,1,0:T(8,128)S(1)} %fusion.39, f32[192,1024]{1,0:T(8,128)S(1)} %get-tuple-element.142, pred[]{:T(512)S(6)} %compare.3), kind=kOutput, calls=%fused_computation.8.clone.1 | convolution fusion | flops 806486016 | bytes 8912901 | tf_op jit(solution)/shard_map/while/body/eval_jaxpr/dot_general | solution.py:76
  239.9 4.0 %fusion.39 = f32[2,192,2048]{2,1,0:T(8,128)S(1)} fusion(bf16[2,192,1024]{2,1,0:T(8,128)(2,1)S(1)} %get-tuple-element.152, bf16[12288,1024]{1,0:T(8,128)(2,1)} %get-tuple-element.151, s32[]{:T(128)S(6)} %select_n.13), kind=kOutput, calls=%fused_computation.5.clone.1 | convolution fusion | flops 1610612736 | bytes 8126468 | tf_op jit(solution)/shard_map/while/body/eval_jaxpr/qoa,ba->qob/dot_general | solution.py:72
  243.9 3.4 %fusion.40 = f32[192,1024]{1,0:T(8,128)S(1)} fusion(bf16[12288,1024]{1,0:T(8,128)(2,1)} %get-tuple-element.151, s32[]{:T(128)S(6)} %select_n.13, f32[2,192,2048]{2,1,0:T(8,128)S(1)} %fusion.39, f32[192,1024]{1,0:T(8,128)S(1)} %get-tuple-element.142, pred[]{:T(512)S(6)} %compare.3), kind=kOutput, calls=%fused_computation.8.clone.1 | convolution fusion | flops 806486016 | bytes 8912901 | tf_op jit(solution)/shard_map/while/body/eval_jaxpr/dot_general | solution.py:76
  247.4 4.0 %fusion.39 = f32[2,192,2048]{2,1,0:T(8,128)S(1)} fusion(bf16[2,192,1024]{2,1,0:T(8,128)(2,1)S(1)} %get-tuple-element.152, bf16[12288,1024]{1,0:T(8,128)(2,1)} %get-tuple-element.151, s32[]{:T(128)S(6)} %select_n.13), kind=kOutput, calls=%fused_computation.5.clone.1 | convolution fusion | flops 1610612736 | bytes 8126468 | tf_op jit(solution)/shard_map/while/body/eval_jaxpr/qoa,ba->qob/dot_general | solution.py:72
  251.4 3.4 %fusion.40 = f32[192,1024]{1,0:T(8,128)S(1)} fusion(bf16[12288,1024]{1,0:T(8,128)(2,1)} %get-tuple-element.151, s32[]{:T(128)S(6)} %select_n.13, f32[2,192,2048]{2,1,0:T(8,128)S(1)} %fusion.39, f32[192,1024]{1,0:T(8,128)S(1)} %get-tuple-element.142, pred[]{:T(512)S(6)} %compare.3), kind=kOutput, calls=%fused_computation.8.clone.1 | convolution fusion | flops 806486016 | bytes 8912901 | tf_op jit(solution)/shard_map/while/body/eval_jaxpr/dot_general | solution.py:76
  254.8 4.0 %fusion.39 = f32[2,192,2048]{2,1,0:T(8,128)S(1)} fusion(bf16[2,192,1024]{2,1,0:T(8,128)(2,1)S(1)} %get-tuple-element.152, bf16[12288,1024]{1,0:T(8,128)(2,1)} %get-tuple-element.151, s32[]{:T(128)S(6)} %select_n.13), kind=kOutput, calls=%fused_computation.5.clone.1 | convolution fusion | flops 1610612736 | bytes 8126468 | tf_op jit(solution)/shard_map/while/body/eval_jaxpr/qoa,ba->qob/dot_general | solution.py:72
  258.8 3.4 %fusion.40 = f32[192,1024]{1,0:T(8,128)S(1)} fusion(bf16[12288,1024]{1,0:T(8,128)(2,1)} %get-tuple-element.151, s32[]{:T(128)S(6)} %select_n.13, f32[2,192,2048]{2,1,0:T(8,128)S(1)} %fusion.39, f32[192,1024]{1,0:T(8,128)S(1)} %get-tuple-element.142, pred[]{:T(512)S(6)} %compare.3), kind=kOutput, calls=%fused_computation.8.clone.1 | convolution fusion | flops 806486016 | bytes 8912901 | tf_op jit(solution)/shard_map/while/body/eval_jaxpr/dot_general | solution.py:76
  262.3 0.2 copy.11
  262.5 0.3 copy.12
  262.8 4.2 %all_to_all.15 = bf16[32,2,1,192,16]{3,0,4,2,1:T(8,128)(2,1)S(1)} all-to-all(bf16[32,2,1,192,16]{3,0,4,2,1:T(8,128)(2,1)S(1)} %copy.12), channel_id=1, replica_groups=mesh['tm'=2,'grid_0'=2,'grid_1'=4,'grid_2'=4,'grid_3'=2] {'grid_3'}, dimensions={1} | all-to-all | bytes 786432 | tf_op jit(solution)/shard_map/all_to_all | solution.py:28
  266.9 1.4 copy.13
  268.3 5.4 %all-to-all-start.1 = ((bf16[32,2,1,192,16]{3,1,4,2,0:T(2,128)(2,1)}), bf16[32,2,1,192,16]{3,1,4,2,0:T(2,128)(2,1)S(1)}, u32[]{:S(2)}, u32[]{:S(2)}) async-start(bf16[32,2,1,192,16]{3,1,4,2,0:T(2,128)(2,1)} %copy.13), calls=%async_computation.1 | async-start | bytes 1048576 | tf_op jit(solution)/shard_map/all_to_all | solution.py:28
  273.8 0.0 copy-done
  273.8 0.2 dynamic-slice_reduce_fusion
  273.9 12.9 %all-to-all-done.1 = bf16[32,2,1,192,16]{3,1,4,2,0:T(2,128)(2,1)S(1)} async-done(((bf16[32,2,1,192,16]{3,1,4,2,0:T(2,128)(2,1)}), bf16[32,2,1,192,16]{3,1,4,2,0:T(2,128)(2,1)S(1)}, u32[]{:S(2)}, u32[]{:S(2)}) %all-to-all-start.1) | async-done | bytes 393248 | tf_op jit(solution)/shard_map/all_to_all | solution.py:28
  286.8 0.5 copy.14
  287.3 0.5 reshape.31
  287.8 9.9 %fusion.25 = f32[16,1024]{1,0:T(8,128)S(1)} fusion(bf16[12288,16]{0,1:T(8,128)(2,1)S(1)} %reshape.31, bf16[12288,1024]{1,0:T(8,128)(2,1)} %get-tuple-element.160), kind=kOutput, calls=%fused_computation.20 | convolution fusion | flops 402653184 | bytes 25624576 | tf_op jit(solution)/shard_map/tsk,sl->tkl/dot_general | solution.py:94
  297.7 0.1 multiply_multiply_fusion
  297.8 6.9 %all_to_all.16 = f32[2,1,16,1024]{3,2,1,0:T(8,128)S(1)} all-to-all(f32[2,1,16,1024]{3,2,1,0:T(8,128)S(1)} %multiply_multiply_fusion), channel_id=1, replica_groups=mesh['tm'=2,'grid_0'=2,'grid_1'=4,'grid_2'=4,'grid_3'=2] {'tm'}, dimensions={0} | all-to-all | bytes 262144 | tf_op jit(solution)/shard_map/all_to_all | solution.py:40
  304.7 0.6 reduce_sum.11
  (1 shorter events, 0.0 us)
Async XLA Ops:
  6.5 267.2 %copy-start = (f32[2,2]{1,0:T(2,128)S(1)}, f32[2,2]{1,0:T(2,128)}, u32[]{:S(2)}) copy-start(f32[2,2]{1,0:T(2,128)} %param.9) | copy-start | bytes 52
  6.5 79.7 %all-gather.5.cloned.1.call-start = ((), (), s32[]{:S(2)}) async-start(), calls=%async_computation.4 | async-start | bytes 4259840 | tf_op jit(solution)/shard_map/all_gather | solution.py:86
  8.0 209.6 %all-gather.3.cloned.1.call-start = ((), (), s32[]{:S(2)}) async-start(), calls=%async_computation.3 | async-start | bytes 25559040 | tf_op jit(solution)/shard_map/all_gather | solution.py:91
  268.3 18.5 %all-to-all-start.1 = ((bf16[32,2,1,192,16]{3,1,4,2,0:T(2,128)(2,1)}), bf16[32,2,1,192,16]{3,1,4,2,0:T(2,128)(2,1)S(1)}, u32[]{:S(2)}, u32[]{:S(2)}) async-start(bf16[32,2,1,192,16]{3,1,4,2,0:T(2,128)(2,1)} %copy.13), calls=%async_computation.1 | async-start | bytes 1048576 | tf_op jit(solution)/shard_map/all_to_all | solution.py:28
Sparse Core Ops, SparseCore 0:
  10.6 75.5 all-gather.4
  89.5 128.0 all-gather.2
where the time goes:
time: 313 us; the launch traced here: 312 us
  waiting for transfers between devices  219 us (70%)
  matrix products  58.1 us (19%)
  between operations  13.5 us (4%)
  blocking collectives  11.1 us (4%)
  starting transfers between devices  5.47 us (2%)
    all_gather x1, waiting for transfers between devices, shards(): lax.all_gather(basis, GRID, axis=0, tiled=True)  128 us
    all_gather x1, waiting for transfers between devices, shards(): lax.all_gather(stacked, GRID, axis=2, tiled=True)  77.5 us
    dot_general x6, matrix products, one_step(): jnp.einsum('qoa,ba->qob', combined_rows, basis_subpart, preferred_element...  24.1 us
    dot_general x6, matrix products, one_step(): jnp.dot(product, basis_subpart, preferred_element_type=jnp.float32)  20.4 us
    all_to_all x1, waiting for transfers between devices, moved_by_axis(): lax.all_to_all(tiles, axes[k], split_axis=k, concat_axis=k, tiled=True)  12.9 us
    dot_general x1, matrix products, shards(): jnp.einsum('tsk,sl->tkl', columns, lax.all_gather(basis, GRID, axis=0, ti...  9.89 us
    all_to_all x1, blocking collectives, sent_and_summed(): lax.all_to_all(tiles, axis, split_axis=0, concat_axis=0, tiled=True)  6.9 us
  transfers between devices with their start and end apart: 3, of which 3 were waited for; matrix products, arithmetic and copies ran while one was open for 1% of the time, Pallas kernels for 0%

commit v1 on v0

--- a/solution.py
+++ b/solution.py
@@ -83,7 +83,9 @@
     projected = jnp.einsum(
         "sl,ftkl->ftsk",
         basis,
-        lax.all_gather(stacked, GRID, axis=2, tiled=True),
+        jnp.concatenate(
+            lax.all_to_all(jnp.stack([stacked] * lax.axis_size(GRID)), GRID, 0, 0), axis=2
+        ),
         preferred_element_type=jnp.float32,
     ).astype(jnp.bfloat16)
     combined_rows = projected.reshape(2, time_count * row_total, NB)

time: 313 us -> 298 us (0.952)
  waiting for transfers between devices: 219 us -> 174 us
  matrix products: 58.1 us -> 71.6 us
  starting transfers between devices: 5.47 us -> 17 us
  local copies, waits for them, and re-layouts: 3.09 us -> 8.24 us
    all_gather x1 -> x0, waiting for transfers between devices: 77.5 us -> none  [shards(): lax.all_gather(stacked, GRID, axis=2, tiled=True)]
    all_to_all x0 -> x1, waiting for transfers between devices: none -> 56.1 us  [shards(): lax.all_to_all(jnp.stack([stacked] * lax.axis_size(GRID)), GRID, 0, 0)]
    all_gather x1, waiting for transfers between devices: 128 us -> 104 us  [shards(): lax.all_gather(basis, GRID, axis=0, tiled=True)]
    all_to_all x0 -> x1, starting transfers between devices: none -> 11.6 us  [shards(): lax.all_to_all(jnp.stack([stacked] * lax.axis_size(GRID)), GRID, 0, 0)]
    dot_general x6, matrix products: 24.1 us -> 34.5 us  [one_step(): jnp.einsum('qoa,ba->qob', combined_rows, basis_subpart, preferred_element...]
    dot_general x6, matrix products: 20.4 us -> 25.7 us  [one_step(): jnp.dot(product, basis_subpart, preferred_element_type=jnp.float32)]
  transfers between devices with their start and end apart: 3 -> 3, of which waited for: 3 -> 3; matrix products, arithmetic and copies ran while one was open for 1% -> 3% of each run, Pallas kernels for 0% -> 0%
where the time goes in v1:
time: 298 us; the launch traced here: 297 us
  waiting for transfers between devices  174 us (58%)
  matrix products  71.6 us (24%)
  starting transfers between devices  17 us (6%)
  between operations  13.5 us (5%)
  blocking collectives  11.1 us (4%)
  local copies, waits for them, and re-layouts  8.24 us (3%)
    all_gather x1, waiting for transfers between devices, shards(): lax.all_gather(basis, GRID, axis=0, tiled=True)  104 us
    all_to_all x1, waiting for transfers between devices, shards(): lax.all_to_all(jnp.stack([stacked] * lax.axis_size(GRID)), GRID, 0, 0)  56.1 us
    dot_general x6, matrix products, one_step(): jnp.einsum('qoa,ba->qob', combined_rows, basis_subpart, preferred_element...  34.5 us
    dot_general x6, matrix products, one_step(): jnp.dot(product, basis_subpart, preferred_element_type=jnp.float32)  25.7 us
    all_to_all x1, waiting for transfers between devices, moved_by_axis(): lax.all_to_all(tiles, axes[k], split_axis=k, concat_axis=k, tiled=True)  12.9 us
    all_to_all x1, starting transfers between devices, shards(): lax.all_to_all(jnp.stack([stacked] * lax.axis_size(GRID)), GRID, 0, 0)  11.6 us
    dot_general x1, matrix products, shards(): jnp.einsum('tsk,sl->tkl', columns, lax.all_gather(basis, GRID, axis=0, ti...  9.89 us
    all_to_all x1, blocking collectives, sent_and_summed(): lax.all_to_all(tiles, axis, split_axis=0, concat_axis=0, tiled=True)  6.91 us
  transfers between devices with their start and end apart: 3, of which 3 were waited for; matrix products, arithmetic and copies ran while one was open for 3% of the time, Pallas kernels for 0%

profile of v1, /device:TPU:0, one launch (start us, length us, event | category | flops | bytes accessed | tf_op | source)
XLA Modules:
  0.0 297.3 jit_solution(16287569648246031915)
XLA Ops:
  6.5 0.0 copy-start
  6.5 0.0 all-gather.2.cloned.1.call-start
  6.5 0.7 all-gather.2.cloned.1.call-update
  7.3 0.8 maximum_bitcast_fusion
  8.0 2.5 stack.14
  10.5 11.6 %all-to-all-start = ((bf16[64,2,1,16,1024]{4,3,1,2,0:T(8,128)(2,1)}), bf16[64,2,1,16,1024]{4,3,1,2,0:T(8,128)(2,1)}, u32[]{:S(2)}, u32[]{:S(2)}) async-start(bf16[64,2,1,16,1024]{4,3,1,2,0:T(8,128)(2,1)} %stack.14), calls=%async_computation | async-start | bytes 8388608 | tf_op jit(solution)/shard_map/all_to_all | solution.py:87
  22.2 56.1 %all-to-all-done = bf16[64,2,1,16,1024]{4,3,1,2,0:T(8,128)(2,1)} async-done(((bf16[64,2,1,16,1024]{4,3,1,2,0:T(8,128)(2,1)}), bf16[64,2,1,16,1024]{4,3,1,2,0:T(8,128)(2,1)}, u32[]{:S(2)}, u32[]{:S(2)}) %all-to-all-start) | async-done | bytes 4194336 | tf_op jit(solution)/shard_map/all_to_all | solution.py:87
  78.3 0.0 copy-start.1
  78.3 2.7 copy.12
  81.0 0.0 copy-done.1
  81.0 1.5 fusion.16
  82.5 104.5 %all-gather.2.cloned.1.call-done = bf16[12288,1024]{1,0:T(8,128)(2,1)} async-done(((bf16[192,1024]{1,0:T(8,128)(2,1)}), bf16[12288,1024]{1,0:T(8,128)(2,1)}) %all-gather.2.cloned.1.call-update) | async-done | bytes 25165840 | tf_op jit(solution)/shard_map/all_gather | solution.py:93
  187.0 60.4 %while.14 = (s32[]{:T(128)}, f32[192,1024]{1,0:T(8,128)S(1)}, bf16[12288,1024]{1,0:T(8,128)(2,1)}, bf16[2,192,1024]{2,1,0:T(8,128)(2,1)S(1)}, s32[]{:T(128)}, /*index=5*/s32[]{:T(128)}, s32[]{:T(128)}, s32[]{:T(128)}) while((s32[]{:T(128)}, f32[192,1024]{1,0:T(8,128)S(1)}, bf16[12288,1024]{1,0:T(8,128)(2,1)}, ...), condition=%wide.region_1.0_spmd.clone, body=%wide.region_0.0_spmd.clone.sunk | while | flops 2417098752 | bytes 17039508 | solution.py:78
  187.0 5.7 %fusion.33 = f32[2,192,2048]{2,1,0:T(8,128)} fusion(bf16[2,192,1024]{2,1,0:T(8,128)(2,1)S(1)} %get-tuple-element.152, bf16[12288,1024]{1,0:T(8,128)(2,1)} %get-tuple-element.151, s32[]{:T(128)S(6)} %select_n.13), kind=kOutput, calls=%fused_computation.5.clone.1 | convolution fusion | flops 1610612736 | bytes 8126468 | tf_op jit(solution)/shard_map/while/body/eval_jaxpr/qoa,ba->qob/dot_general | solution.py:72
  192.8 4.3 %fusion.34 = f32[192,1024]{1,0:T(8,128)S(1)} fusion(bf16[12288,1024]{1,0:T(8,128)(2,1)} %get-tuple-element.151, s32[]{:T(128)S(6)} %select_n.13, f32[2,192,2048]{2,1,0:T(8,128)} %fusion.33, f32[192,1024]{1,0:T(8,128)S(1)} %get-tuple-element.142, pred[]{:T(512)S(6)} %compare.3), kind=kOutput, calls=%fused_computation.8.clone.1 | convolution fusion | flops 806486016 | bytes 8912901 | tf_op jit(solution)/shard_map/while/body/eval_jaxpr/dot_general | solution.py:76
  197.1 5.7 %fusion.33 = f32[2,192,2048]{2,1,0:T(8,128)} fusion(bf16[2,192,1024]{2,1,0:T(8,128)(2,1)S(1)} %get-tuple-element.152, bf16[12288,1024]{1,0:T(8,128)(2,1)} %get-tuple-element.151, s32[]{:T(128)S(6)} %select_n.13), kind=kOutput, calls=%fused_computation.5.clone.1 | convolution fusion | flops 1610612736 | bytes 8126468 | tf_op jit(solution)/shard_map/while/body/eval_jaxpr/qoa,ba->qob/dot_general | solution.py:72
  202.8 4.3 %fusion.34 = f32[192,1024]{1,0:T(8,128)S(1)} fusion(bf16[12288,1024]{1,0:T(8,128)(2,1)} %get-tuple-element.151, s32[]{:T(128)S(6)} %select_n.13, f32[2,192,2048]{2,1,0:T(8,128)} %fusion.33, f32[192,1024]{1,0:T(8,128)S(1)} %get-tuple-element.142, pred[]{:T(512)S(6)} %compare.3), kind=kOutput, calls=%fused_computation.8.clone.1 | convolution fusion | flops 806486016 | bytes 8912901 | tf_op jit(solution)/shard_map/while/body/eval_jaxpr/dot_general | solution.py:76
  207.1 5.7 %fusion.33 = f32[2,192,2048]{2,1,0:T(8,128)} fusion(bf16[2,192,1024]{2,1,0:T(8,128)(2,1)S(1)} %get-tuple-element.152, bf16[12288,1024]{1,0:T(8,128)(2,1)} %get-tuple-element.151, s32[]{:T(128)S(6)} %select_n.13), kind=kOutput, calls=%fused_computation.5.clone.1 | convolution fusion | flops 1610612736 | bytes 8126468 | tf_op jit(solution)/shard_map/while/body/eval_jaxpr/qoa,ba->qob/dot_general | solution.py:72
  212.9 4.3 %fusion.34 = f32[192,1024]{1,0:T(8,128)S(1)} fusion(bf16[12288,1024]{1,0:T(8,128)(2,1)} %get-tuple-element.151, s32[]{:T(128)S(6)} %select_n.13, f32[2,192,2048]{2,1,0:T(8,128)} %fusion.33, f32[192,1024]{1,0:T(8,128)S(1)} %get-tuple-element.142, pred[]{:T(512)S(6)} %compare.3), kind=kOutput, calls=%fused_computation.8.clone.1 | convolution fusion | flops 806486016 | bytes 8912901 | tf_op jit(solution)/shard_map/while/body/eval_jaxpr/dot_general | solution.py:76
  217.2 5.7 %fusion.33 = f32[2,192,2048]{2,1,0:T(8,128)} fusion(bf16[2,192,1024]{2,1,0:T(8,128)(2,1)S(1)} %get-tuple-element.152, bf16[12288,1024]{1,0:T(8,128)(2,1)} %get-tuple-element.151, s32[]{:T(128)S(6)} %select_n.13), kind=kOutput, calls=%fused_computation.5.clone.1 | convolution fusion | flops 1610612736 | bytes 8126468 | tf_op jit(solution)/shard_map/while/body/eval_jaxpr/qoa,ba->qob/dot_general | solution.py:72
  222.9 4.3 %fusion.34 = f32[192,1024]{1,0:T(8,128)S(1)} fusion(bf16[12288,1024]{1,0:T(8,128)(2,1)} %get-tuple-element.151, s32[]{:T(128)S(6)} %select_n.13, f32[2,192,2048]{2,1,0:T(8,128)} %fusion.33, f32[192,1024]{1,0:T(8,128)S(1)} %get-tuple-element.142, pred[]{:T(512)S(6)} %compare.3), kind=kOutput, calls=%fused_computation.8.clone.1 | convolution fusion | flops 806486016 | bytes 8912901 | tf_op jit(solution)/shard_map/while/body/eval_jaxpr/dot_general | solution.py:76
  227.3 5.7 %fusion.33 = f32[2,192,2048]{2,1,0:T(8,128)} fusion(bf16[2,192,1024]{2,1,0:T(8,128)(2,1)S(1)} %get-tuple-element.152, bf16[12288,1024]{1,0:T(8,128)(2,1)} %get-tuple-element.151, s32[]{:T(128)S(6)} %select_n.13), kind=kOutput, calls=%fused_computation.5.clone.1 | convolution fusion | flops 1610612736 | bytes 8126468 | tf_op jit(solution)/shard_map/while/body/eval_jaxpr/qoa,ba->qob/dot_general | solution.py:72
  233.0 4.3 %fusion.34 = f32[192,1024]{1,0:T(8,128)S(1)} fusion(bf16[12288,1024]{1,0:T(8,128)(2,1)} %get-tuple-element.151, s32[]{:T(128)S(6)} %select_n.13, f32[2,192,2048]{2,1,0:T(8,128)} %fusion.33, f32[192,1024]{1,0:T(8,128)S(1)} %get-tuple-element.142, pred[]{:T(512)S(6)} %compare.3), kind=kOutput, calls=%fused_computation.8.clone.1 | convolution fusion | flops 806486016 | bytes 8912901 | tf_op jit(solution)/shard_map/while/body/eval_jaxpr/dot_general | solution.py:76
  237.3 5.7 %fusion.33 = f32[2,192,2048]{2,1,0:T(8,128)} fusion(bf16[2,192,1024]{2,1,0:T(8,128)(2,1)S(1)} %get-tuple-element.152, bf16[12288,1024]{1,0:T(8,128)(2,1)} %get-tuple-element.151, s32[]{:T(128)S(6)} %select_n.13), kind=kOutput, calls=%fused_computation.5.clone.1 | convolution fusion | flops 1610612736 | bytes 8126468 | tf_op jit(solution)/shard_map/while/body/eval_jaxpr/qoa,ba->qob/dot_general | solution.py:72
  243.1 4.3 %fusion.34 = f32[192,1024]{1,0:T(8,128)S(1)} fusion(bf16[12288,1024]{1,0:T(8,128)(2,1)} %get-tuple-element.151, s32[]{:T(128)S(6)} %select_n.13, f32[2,192,2048]{2,1,0:T(8,128)} %fusion.33, f32[192,1024]{1,0:T(8,128)S(1)} %get-tuple-element.142, pred[]{:T(512)S(6)} %compare.3), kind=kOutput, calls=%fused_computation.8.clone.1 | convolution fusion | flops 806486016 | bytes 8912901 | tf_op jit(solution)/shard_map/while/body/eval_jaxpr/dot_general | solution.py:76
  247.4 0.2 copy.13
  247.6 0.3 copy.14
  247.9 4.2 %all_to_all.20 = bf16[32,2,1,192,16]{3,0,4,2,1:T(8,128)(2,1)S(1)} all-to-all(bf16[32,2,1,192,16]{3,0,4,2,1:T(8,128)(2,1)S(1)} %copy.14), channel_id=1, replica_groups=mesh['tm'=2,'grid_0'=2,'grid_1'=4,'grid_2'=4,'grid_3'=2] {'grid_3'}, dimensions={1} | all-to-all | bytes 786432 | tf_op jit(solution)/shard_map/all_to_all | solution.py:28
  252.0 1.4 copy.15
  253.4 5.4 %all-to-all-start.2 = ((bf16[32,2,1,192,16]{3,1,4,2,0:T(2,128)(2,1)}), bf16[32,2,1,192,16]{3,1,4,2,0:T(2,128)(2,1)S(1)}, u32[]{:S(2)}, u32[]{:S(2)}) async-start(bf16[32,2,1,192,16]{3,1,4,2,0:T(2,128)(2,1)} %copy.15), calls=%async_computation.2 | async-start | bytes 1048576 | tf_op jit(solution)/shard_map/all_to_all | solution.py:28
  258.9 0.0 copy-done
  258.9 0.2 dynamic-slice_reduce_fusion
  259.1 12.9 %all-to-all-done.2 = bf16[32,2,1,192,16]{3,1,4,2,0:T(2,128)(2,1)S(1)} async-done(((bf16[32,2,1,192,16]{3,1,4,2,0:T(2,128)(2,1)}), bf16[32,2,1,192,16]{3,1,4,2,0:T(2,128)(2,1)S(1)}, u32[]{:S(2)}, u32[]{:S(2)}) %all-to-all-start.2) | async-done | bytes 393248 | tf_op jit(solution)/shard_map/all_to_all | solution.py:28
  271.9 0.5 copy.16
  272.4 0.5 reshape.40
  273.0 9.9 %fusion.18 = f32[16,1024]{1,0:T(8,128)S(1)} fusion(bf16[12288,16]{0,1:T(8,128)(2,1)S(1)} %reshape.40, bf16[12288,1024]{1,0:T(8,128)(2,1)} %get-tuple-element.159), kind=kOutput, calls=%fused_computation.18 | convolution fusion | flops 402653184 | bytes 25624576 | tf_op jit(solution)/shard_map/tsk,sl->tkl/dot_general | solution.py:96
  282.8 0.1 multiply_multiply_fusion
  282.9 6.9 %all_to_all.21 = f32[2,1,16,1024]{3,2,1,0:T(8,128)S(1)} all-to-all(f32[2,1,16,1024]{3,2,1,0:T(8,128)S(1)} %multiply_multiply_fusion), channel_id=1, replica_groups=mesh['tm'=2,'grid_0'=2,'grid_1'=4,'grid_2'=4,'grid_3'=2] {'tm'}, dimensions={0} | all-to-all | bytes 262144 | tf_op jit(solution)/shard_map/all_to_all | solution.py:40
  289.9 0.6 reduce_sum.11
  (1 shorter events, 0.0 us)
Async XLA Ops:
  6.5 252.3 %copy-start = (f32[2,2]{1,0:T(2,128)S(1)}, f32[2,2]{1,0:T(2,128)}, u32[]{:S(2)}) copy-start(f32[2,2]{1,0:T(2,128)} %param.9) | copy-start | bytes 52
  6.5 180.5 %all-gather.2.cloned.1.call-start = ((), (), s32[]{:S(2)}) async-start(), calls=%async_computation.4 | async-start | bytes 25559040 | tf_op jit(solution)/shard_map/all_gather | solution.py:93
  10.5 67.8 %all-to-all-start = ((bf16[64,2,1,16,1024]{4,3,1,2,0:T(8,128)(2,1)}), bf16[64,2,1,16,1024]{4,3,1,2,0:T(8,128)(2,1)}, u32[]{:S(2)}, u32[]{:S(2)}) async-start(bf16[64,2,1,16,1024]{4,3,1,2,0:T(8,128)(2,1)} %stack.14), calls=%async_computation | async-start | bytes 8388608 | tf_op jit(solution)/shard_map/all_to_all | solution.py:87
  78.3 2.7 copy-start.1
  253.4 18.5 %all-to-all-start.2 = ((bf16[32,2,1,192,16]{3,1,4,2,0:T(2,128)(2,1)}), bf16[32,2,1,192,16]{3,1,4,2,0:T(2,128)(2,1)S(1)}, u32[]{:S(2)}, u32[]{:S(2)}) async-start(bf16[32,2,1,192,16]{3,1,4,2,0:T(2,128)(2,1)} %copy.15), calls=%async_computation.2 | async-start | bytes 1048576 | tf_op jit(solution)/shard_map/all_to_all | solution.py:28
Sparse Core Ops, SparseCore 0:
  10.6 176.3 all-gather.1
